TPU v7x, 256 devices: a whole 4x4x8 slice. The times are simulated.
256 devices in a mesh: sub: 4 (over x), row: 4 (over y_lo, core), col: 16 (over z, y_hi).
Axes of the slice: x: 4, y: 4 (y_hi: 2, y_lo: 2; y = y_hi * 2 + y_lo), z: 8, core: 2. Of those that a mesh axis runs over, the one named last changes fastest.
Arguments:
- leaf_sizes: int32 [512], P(('sub', 'row', 'col')), may hold values from 20 to 219
- remap: int32 [4], replicated, may hold values from 0 to 3, each once
- panel_diag: float32 [4, 1536, 1536], P('sub', ('row', 'col')), may hold values from -1 to 6, as said below
- panel_below: float32 [4, 5632, 1536], P('sub', ('row', 'col')), may hold values from -1.2 to 1.2
- trailing: float32 [4, 5632, 5632], P('sub', 'row', 'col'), may hold values from -6 to 26, as said below
Outputs:
- diag_factor: float32 [4, 1536, 1536], P('sub', ('row', 'col'))
- panel_factor: float32 [4, 5632, 1536], P('sub', ('row', 'col'))
- schur: float32 [4, 5632, 5632], P('sub', 'row', 'col')
- subtree_cost: float32 [4], P('sub')
Inputs may be any that keep to these rules, and one draw needn't show every extreme that they name: remap is a permutation: front j moves to subcube remap[j]. `panel_diag`: each front's block is symmetric and positive definite. `trailing`: each front's block is symmetric.
All inputs are finite; a program needn't handle non-finite values.
Results may differ from a plain program's by a relative error of at most 0.0001.
Values sent between devices are 32-bit elements; how exact they have to be, the bound alone decides.
No kernel may reach another device: no remote copies, remote signals or barrier semaphores. Data moves between devices by JAX's collectives and lax.ppermute only.
A program may use at most 128 MiB of HBM per device.

v0:
```python
import jax
import jax.numpy as jnp
from jax import lax
from jax.sharding import Mesh
from jax.sharding import PartitionSpec as P

ROW = ("row_0", "row_1")
COL = ("col_0", "col_1")
ROW_COL = ("row_0", "row_1", "col_0", "col_1")
SUB_ROW_COL = ("sub", "row_0", "row_1", "col_0", "col_1")


def from_everyone(value, axis):
    copies = jnp.broadcast_to(value, (lax.axis_size(axis), *value.shape))
    return lax.all_to_all(copies, axis, split_axis=0, concat_axis=0, tiled=True)


def taken_together(value, axis):
    everything = from_everyone(value, axis)
    return jnp.sum(everything, axis=0)


def in_one_piece(arrays, axis, split_dim, concat_dim, along):
    ends, at = ([], 0)
    for a in arrays[:-1]:
        at += a.shape[along]
        ends.append(at)
    both = jnp.concatenate(arrays, axis=along)
    return tuple(
        jnp.split(
            lax.all_to_all(both, axis, split_axis=split_dim, concat_axis=concat_dim, tiled=True),
            ends,
            axis=along,
        )
    )


def joined_along(pieces, dim):
    shape = list(pieces.shape[1:])
    shape[dim] *= pieces.shape[0]
    return jnp.moveaxis(pieces, 0, dim).reshape(shape)


def gather_in_order(value, axes, order):
    pieces = value[None]
    for k in order:
        pieces = lax.all_gather(pieces, axes[k], axis=0, tiled=True)
    block = [lax.axis_size(axes[k]) for k in reversed(order)]
    pieces = pieces.reshape(*block, *value.shape)
    turned = sorted(range(len(order)), key=lambda place: order[len(order) - 1 - place])
    return pieces.transpose(*turned, *range(len(order), pieces.ndim)).reshape(-1, *value.shape)


def gather_axes(value, axes, order, dim):
    return joined_along(gather_in_order(value, axes, order), dim)


def broadcast(value, axis, root):
    return lax.dynamic_index_in_dim(lax.all_gather(value, axis), root, 0, keepdims=False)


def column_rows(row_block, rows_count, cols_count, column, sender):
    block_rows = row_block.shape[0]
    col_rows = block_rows * rows_count // cols_count
    per_part = min(col_rows, block_rows)
    begin_row = column * col_rows + 0
    holder = begin_row // block_rows
    offset = begin_row % block_rows
    pieces = sender(lax.dynamic_slice_in_dim(row_block, offset, per_part, 0), holder)
    return pieces


def local(leaf_sizes, remap, panel_diag, panel_below, trailing):
    rows_count = lax.axis_size(ROW)
    cols_count = lax.axis_size(COL)
    scaled = leaf_sizes.astype(jnp.float32) / 100.0
    partial_cost = jnp.sum(scaled * scaled * scaled)
    summed = taken_together(partial_cost, ROW_COL)
    subtree_cost = jnp.reshape(summed / (leaf_sizes.shape[0] * rows_count * cols_count), (1,))
    front_count = remap.shape[0]
    counter = jnp.arange(front_count, dtype=jnp.int32)
    sources = jnp.sum(
        counter[None, :] * (remap[None, :] == counter[:, None]).astype(jnp.int32), axis=1
    )
    spread = (
        *in_one_piece((panel_diag, panel_below), "sub", 2, 0, 1),
        lax.all_to_all(trailing, "sub", split_axis=2, concat_axis=0, tiled=True),
    )
    ordered = (
        jnp.take(spread[0], sources, axis=0),
        jnp.take(spread[1], sources, axis=0),
        jnp.take(spread[2], sources, axis=0),
    )
    mine = (
        *in_one_piece((ordered[0], ordered[1]), "sub", 0, 2, 1),
        lax.all_to_all(ordered[2], "sub", split_axis=0, concat_axis=2, tiled=True),
    )
    diag_block = mine[0][0]
    below_block = mine[1][0]
    trail_block = mine[2][0]
    gathered = gather_axes(diag_block, ROW_COL, (3, 0, 2, 1), 0)
    factor_low = jnp.linalg.cholesky(gathered)
    column = lax.axis_index(COL)
    flat_index = lax.axis_index(ROW) * cols_count + column
    diag_count = diag_block.shape[0]
    diag_factor = lax.dynamic_slice_in_dim(factor_low, flat_index * diag_count, diag_count, 0)
    own_rows = lax.linalg.triangular_solve(
        factor_low, below_block, left_side=False, lower=True, transpose_a=True
    )
    row_block = lax.all_gather(own_rows, COL, axis=0, tiled=True)
    col_block = column_rows(
        row_block,
        rows_count,
        cols_count,
        column,
        lambda block_part, root_index: broadcast(block_part, ROW, root_index),
    )
    update = lax.dot_general(
        row_block,
        col_block,
        (((1,), (1,)), ((), ())),
        precision=lax.Precision.HIGHEST,
        preferred_element_type=jnp.float32,
    )
    schur_block = trail_block - update
    return (diag_factor[None], own_rows[None], schur_block[None], subtree_cost)


def solution(mesh):
    finer = Mesh(
        mesh.devices.reshape(mesh.shape["sub"], 2, 2, 8, 2),
        ("sub", "row_0", "row_1", "col_0", "col_1"),
    )
    return jax.shard_map(
        local,
        mesh=finer,
        in_specs=(
            P(SUB_ROW_COL),
            P(),
            P("sub", ROW_COL, None),
            P("sub", ROW_COL, None),
            P("sub", ROW, COL),
        ),
        out_specs=(P("sub", ROW_COL, None), P("sub", ROW_COL, None), P("sub", ROW, COL), P("sub")),
        check_vma=False,
    )
```

profile of v0, /device:TPU:1, one launch (start us, length us, event | category | flops | bytes accessed | tf_op | source)
XLA Modules:
  0.0 948.4 jit_solution(2037040901221429000)
XLA Ops:
  10.0 4.8 all-to-all-start
  15.7 9.5 all-to-all-done
  26.8 10.4 %all_to_all.75 = f32[4,112,384]{2,1,0:T(8,128)S(1)} all-to-all(f32[4,112,384]{2,1,0:T(8,128)S(1)} %pad_maximum_fusion.1), channel_id=1, replica_groups=mesh['sub'=4,'row_0'=2,'row_1'=2,'col_0'=8,'col_1'=2] {'sub'}, dimensions={0} | all-to-all | bytes 1376256 | tf_op jit(solution)/shard_map/all_to_all | solution.py:31
  37.4 8.7 all_gather.21
  46.1 6.8 all_gather.22
  53.0 64.9 %all-gather.6.cloned.1.call-done = f32[32,24,1536]{2,1,0:T(8,128)} async-done(((f32[4,24,1536]{2,1,0:T(8,128)}), f32[32,24,1536]{2,1,0:T(8,128)}) %all-gather.6.cloned.1.call-update) | async-done | bytes 4718608 | tf_op jit(solution)/shard_map/all_gather | solution.py:47
  118.0 28.2 %all-gather.8.cloned.1.call-done = f32[64,24,1536]{2,1,0:T(8,128)} async-done(((f32[32,24,1536]{2,1,0:T(8,128)}), f32[64,24,1536]{2,1,0:T(8,128)}) %all-gather.8.cloned.1.call-update) | async-done | bytes 9437200 | tf_op jit(solution)/shard_map/all_gather | solution.py:47
  146.2 8.8 copy.42
  155.0 10.1 %copy.43 = f32[1536,1536]{0,1:T(8,128)} copy(f32[1536,1536]{1,0:T(8,128)} %bitcast.191) | data formatting | bytes 18874368 | tf_op jit(solution)/shard_map/reshape;reshape | solution.py:41
  165.1 12.3 %fusion = f32[1536,1536]{1,0:T(8,128)} fusion(f32[1536,1536]{0,1:T(8,128)} %copy.43, f32[2,2,8,2,24,1536]{5,4,3,2,1,0:T(8,128)} %copy.42), kind=kLoop, calls=%fused_computation.6 | loop fusion | flops 4718592 | bytes 28311552 | tf_op jit(solution)/shard_map/jit(cholesky)/div | solution.py:102
  178.2 11.7 %cholesky.341 = f32[128,128]{1,0:T(8,128)S(1)} custom-call(f32[128,128]{1,0:T(8,128)S(1)} %cholesky.892), custom_call_target="Cholesky" | custom-call | tf_op jit(solution)/shard_map/jit(cholesky)/cholesky | solution.py:102
  190.0 4.9 cholesky.371
  194.9 9.8 %custom-call.94 = f32[1,128,128]{1,2,0:T(8,128)S(1)} custom-call(f32[1,128,128]{2,1,0:T(8,128)S(1)} %get-tuple-element.57), custom_call_target="InvertDiagBlocksLowerTriangular" | custom-call | tf_op jit(solution)/shard_map/jit(cholesky)/cholesky | solution.py:102
  209.4 11.9 %cholesky.362 = f32[128,128]{1,0:T(8,128)S(1)} custom-call(f32[128,128]{1,0:T(8,128)S(1)} %cholesky.896), custom_call_target="Cholesky" | custom-call | tf_op jit(solution)/shard_map/jit(cholesky)/cholesky | solution.py:102
  221.9 9.8 %custom-call.95 = f32[1,128,128]{1,2,0:T(8,128)S(1)} custom-call(f32[1,128,128]{2,1,0:T(8,128)S(1)} %get-tuple-element.54), custom_call_target="InvertDiagBlocksLowerTriangular" | custom-call | tf_op jit(solution)/shard_map/jit(cholesky)/cholesky | solution.py:102
  236.1 11.7 %cholesky.385 = f32[128,128]{1,0:T(8,128)S(1)} custom-call(f32[128,128]{1,0:T(8,128)S(1)} %cholesky.901), custom_call_target="Cholesky" | custom-call | tf_op jit(solution)/shard_map/jit(cholesky)/cholesky | solution.py:102
  248.5 10.0 %custom-call.96 = f32[1,128,128]{1,2,0:T(8,128)S(1)} custom-call(f32[1,128,128]{2,1,0:T(8,128)S(1)} %get-tuple-element.51), custom_call_target="InvertDiagBlocksLowerTriangular" | custom-call | tf_op jit(solution)/shard_map/jit(cholesky)/cholesky | solution.py:102
  263.3 11.7 %cholesky.715 = f32[128,128]{1,0:T(8,128)S(1)} custom-call(f32[128,128]{1,0:T(8,128)S(1)} %cholesky.906), custom_call_target="Cholesky" | custom-call | tf_op jit(solution)/shard_map/jit(cholesky)/cholesky | solution.py:102
  275.7 9.8 %custom-call.97 = f32[1,128,128]{1,2,0:T(8,128)S(1)} custom-call(f32[1,128,128]{2,1,0:T(8,128)S(1)} %get-tuple-element.48), custom_call_target="InvertDiagBlocksLowerTriangular" | custom-call | tf_op jit(solution)/shard_map/jit(cholesky)/cholesky | solution.py:102
  290.6 12.1 %cholesky.734 = f32[128,128]{1,0:T(8,128)S(1)} custom-call(f32[128,128]{1,0:T(8,128)S(1)} %cholesky.911), custom_call_target="Cholesky" | custom-call | tf_op jit(solution)/shard_map/jit(cholesky)/cholesky | solution.py:102
  303.3 9.8 %custom-call.98 = f32[1,128,128]{1,2,0:T(8,128)S(1)} custom-call(f32[1,128,128]{2,1,0:T(8,128)S(1)} %get-tuple-element.45), custom_call_target="InvertDiagBlocksLowerTriangular" | custom-call | tf_op jit(solution)/shard_map/jit(cholesky)/cholesky | solution.py:102
  314.5 3.9 fusion.24
  318.4 11.7 %cholesky.754 = f32[128,128]{1,0:T(8,128)S(1)} custom-call(f32[128,128]{1,0:T(8,128)S(1)} %cholesky.916), custom_call_target="Cholesky" | custom-call | tf_op jit(solution)/shard_map/jit(cholesky)/cholesky | solution.py:102
  330.7 10.0 %custom-call.99 = f32[1,128,128]{1,2,0:T(8,128)S(1)} custom-call(f32[1,128,128]{2,1,0:T(8,128)S(1)} %get-tuple-element.42), custom_call_target="InvertDiagBlocksLowerTriangular" | custom-call | tf_op jit(solution)/shard_map/jit(cholesky)/cholesky | solution.py:102
  341.9 3.8 fusion.27
  345.8 11.7 %cholesky.774 = f32[128,128]{1,0:T(8,128)S(1)} custom-call(f32[128,128]{1,0:T(8,128)S(1)} %cholesky.921), custom_call_target="Cholesky" | custom-call | tf_op jit(solution)/shard_map/jit(cholesky)/cholesky | solution.py:102
  358.1 9.8 %custom-call.100 = f32[1,128,128]{1,2,0:T(8,128)S(1)} custom-call(f32[1,128,128]{2,1,0:T(8,128)S(1)} %get-tuple-element.39), custom_call_target="InvertDiagBlocksLowerTriangular" | custom-call | tf_op jit(solution)/shard_map/jit(cholesky)/cholesky | solution.py:102
  369.1 4.0 fusion.30
  373.2 11.7 %cholesky.794 = f32[128,128]{1,0:T(8,128)S(1)} custom-call(f32[128,128]{1,0:T(8,128)S(1)} %cholesky.926), custom_call_target="Cholesky" | custom-call | tf_op jit(solution)/shard_map/jit(cholesky)/cholesky | solution.py:102
  385.5 9.8 %custom-call.101 = f32[1,128,128]{1,2,0:T(8,128)S(1)} custom-call(f32[1,128,128]{2,1,0:T(8,128)S(1)} %get-tuple-element.36), custom_call_target="InvertDiagBlocksLowerTriangular" | custom-call | tf_op jit(solution)/shard_map/jit(cholesky)/cholesky | solution.py:102
  400.1 12.1 %cholesky.814 = f32[128,128]{1,0:T(8,128)S(1)} custom-call(f32[128,128]{1,0:T(8,128)S(1)} %cholesky.931), custom_call_target="Cholesky" | custom-call | tf_op jit(solution)/shard_map/jit(cholesky)/cholesky | solution.py:102
  412.8 9.8 %custom-call.102 = f32[1,128,128]{1,2,0:T(8,128)S(1)} custom-call(f32[1,128,128]{2,1,0:T(8,128)S(1)} %get-tuple-element.33), custom_call_target="InvertDiagBlocksLowerTriangular" | custom-call | tf_op jit(solution)/shard_map/jit(cholesky)/cholesky | solution.py:102
  426.9 11.7 %cholesky.834 = f32[128,128]{1,0:T(8,128)S(1)} custom-call(f32[128,128]{1,0:T(8,128)S(1)} %cholesky.936), custom_call_target="Cholesky" | custom-call | tf_op jit(solution)/shard_map/jit(cholesky)/cholesky | solution.py:102
  439.3 9.8 %custom-call.103 = f32[1,128,128]{1,2,0:T(8,128)S(1)} custom-call(f32[1,128,128]{2,1,0:T(8,128)S(1)} %get-tuple-element.30), custom_call_target="InvertDiagBlocksLowerTriangular" | custom-call | tf_op jit(solution)/shard_map/jit(cholesky)/cholesky | solution.py:102
  452.8 11.9 %cholesky.854 = f32[128,128]{1,0:T(8,128)S(1)} custom-call(f32[128,128]{1,0:T(8,128)S(1)} %cholesky.941), custom_call_target="Cholesky" | custom-call | tf_op jit(solution)/shard_map/jit(cholesky)/cholesky | solution.py:102
  465.3 9.8 %custom-call.104 = f32[1,128,128]{1,2,0:T(8,128)S(1)} custom-call(f32[1,128,128]{2,1,0:T(8,128)S(1)} %get-tuple-element.27), custom_call_target="InvertDiagBlocksLowerTriangular" | custom-call | tf_op jit(solution)/shard_map/jit(cholesky)/cholesky | solution.py:102
  478.2 11.7 %cholesky.872 = f32[128,128]{1,0:T(8,128)S(1)} custom-call(f32[128,128]{1,0:T(8,128)S(1)} %convolution_subtract_fusion.4), custom_call_target="Cholesky" | custom-call | tf_op jit(solution)/shard_map/jit(cholesky)/cholesky | solution.py:102
  505.4 13.0 %fusion.1 = (f32[1536,1536]{1,0:T(8,128)}, f32[1536,1536]{1,0:T(8,128)}) fusion(f32[1536,1536]{1,0:T(8,128)} %get-tuple-element.25, pred[]{:T(512)S(6)} %cholesky.891), kind=kLoop, calls=%fused_computation.9 | loop fusion | flops 9437184 | bytes 28311552 | tf_op jit(solution)/shard_map/triangular_solve | solution.py:107
  518.4 34.8 %while.1 = (s32[]{:T(128)}, f32[1536,1536]{1,0:T(8,128)}, s32[12,2]{0,1:T(2,128)S(1)}, f32[12,128,128]{2,1,0:T(8,128)S(1)}, s32[]{:T(128)}) while((s32[]{:T(128)}, f32[1536,1536]{1,0:T(8,128)}, s32[12,2]{0,1:T(2,128)S(1)}, f32[12,128,128]{2,1,0:T(8,128)S(1)}, s32[]{:T(128)}) %tuple.108), condition=%wide.while_cond, body=%wide.while_body.sunk | while | flops 2 | bytes 131189 | solution.py:107
  553.3 117.9 %custom-call.105 = f32[12,128,128]{1,2,0:T(8,128)S(1)} custom-call(f32[12,128,128]{2,1,0:T(8,128)S(1)} %get-tuple-element.11), custom_call_target="InvertDiagBlocksLowerTriangular" | custom-call | tf_op jit(solution)/shard_map/triangular_solve | solution.py:107
  700.6 137.7 %all-gather.10.cloned.1.call-done = f32[1408,1536]{1,0:T(8,128)} async-done(((f32[88,1536]{1,0:T(8,128)}), f32[1408,1536]{1,0:T(8,128)}) %all-gather.10.cloned.1.call-update) | async-done | bytes 8650768 | tf_op jit(solution)/shard_map/all_gather | solution.py:110
  844.9 4.0 all-to-all-start.2
  849.4 22.9 %all-to-all-done.2 = f32[1,1408,352]{1,0,2:T(1,128)S(1)} async-done(((f32[1,1408,352]{1,0,2:T(1,128)}), f32[1,1408,352]{1,0,2:T(1,128)S(1)}, u32[]{:S(2)}, u32[]{:S(2)}) %all-to-all-start.2) | async-done | bytes 1982496 | tf_op jit(solution)/shard_map/all_to_all | solution.py:87
  873.6 8.0 all-to-all-start.4
  886.8 3.9 all-to-all-done.4
  897.2 21.3 %all-to-all-done.3 = f32[4,1408,88]{1,2,0:T(8,128)S(1)} async-done(((f32[4,1408,88]{1,2,0:T(8,128)}), f32[4,1408,88]{1,2,0:T(8,128)S(1)}, u32[]{:S(2)}, u32[]{:S(2)}) %all-to-all-start.3) | async-done | bytes 1982496 | tf_op jit(solution)/shard_map/all_to_all | solution.py:96
  918.5 7.6 all-gather.12.cloned.1.call-done
  926.1 14.4 %fusion.2 = f32[1,1408,352]{1,2,0:T(8,128)} fusion(f32[1408,352]{0,1:T(8,128)S(1)} %bitcast.193, f32[1408,1536]{1,0:T(8,128)} %all-gather.10.cloned.1.call-done, f32[4,352,1536]{2,1,0:T(8,128)} %bitcast.203, s32[]{:T(128)S(6)} %select_n.67), kind=kOutput, calls=%fused_computation.11 | convolution fusion | flops 9135689728 | bytes 14778372 | tf_op jit(solution)/shard_map/dot_general | solution.py:118
  (158 shorter events, 142.6 us)
Async XLA Ops:
  10.0 15.1 %all-to-all-start = ((f32[1,112,1536]{1,0,2:T(1,128)}), f32[1,112,1536]{1,0,2:T(1,128)S(1)}, u32[]{:S(2)}, u32[]{:S(2)}) async-start(f32[1,112,1536]{1,0,2:T(1,128)} %copy.38), calls=%async_computation | async-start | bytes 1572864 | tf_op jit(solution)/shard_map/all_to_all | solution.py:31
  14.8 103.0 %all-gather.6.cloned.1.call-start = ((), (), s32[]{:S(2)}) async-start(), calls=%async_computation.5 | async-start | bytes 5308416 | tf_op jit(solution)/shard_map/all_gather | solution.py:47
  52.9 93.2 %all-gather.8.cloned.1.call-start = ((), (), s32[]{:S(2)}) async-start(), calls=%async_computation.6 | async-start | bytes 14155776 | tf_op jit(solution)/shard_map/all_gather | solution.py:47
  117.9 720.4 %all-gather.10.cloned.1.call-start = ((), (), s32[]{:S(2)}) async-start(), calls=%async_computation.7 | async-start | bytes 9191424 | tf_op jit(solution)/shard_map/all_gather | solution.py:110
  671.2 1.4 copy-start.1
  672.8 168.8 %copy-start = (f32[1,1408,352]{1,2,0:T(8,128)S(1)}, f32[1,1408,352]{1,2,0:T(8,128)}, u32[]{:S(2)}) copy-start(f32[1,1408,352]{1,2,0:T(8,128)} %param.9) | copy-start | bytes 5947396
  690.7 158.1 %copy-start.3 = (s32[2]{0:T(128)S(1)}, s32[2]{0:T(128)}, u32[]{:S(2)}) copy-start(s32[2]{0:T(128)} %param.5) | copy-start | bytes 28
  699.7 0.8 copy-start.2
  700.5 225.5 %all-gather.12.cloned.1.call-start = ((), (), s32[]{:S(2)}) async-start(), calls=%async_computation.8 | async-start | bytes 10813440 | tf_op jit(solution)/shard_map/all_gather | solution.py:59
  844.9 27.5 %all-to-all-start.2 = ((f32[1,1408,352]{1,0,2:T(1,128)}), f32[1,1408,352]{1,0,2:T(1,128)S(1)}, u32[]{:S(2)}, u32[]{:S(2)}) async-start(f32[1,1408,352]{1,0,2:T(1,128)} %copy.44), calls=%async_computation.2 | async-start | bytes 3964928 | tf_op jit(solution)/shard_map/all_to_all | solution.py:87
  873.6 17.0 %all-to-all-start.4 = ((f32[64,1,1]{2,1,0:T(1,128)}), f32[64,1,1]{2,1,0:T(1,128)S(1)}, u32[]{:S(2)}, u32[]{:S(2)}) async-start(f32[64,1,1]{2,1,0:T(1,128)} %broadcast_in_dim.56), calls=%async_computation.4 | async-start | bytes 65536 | tf_op jit(solution)/shard_map/all_to_all | solution.py:15
  890.7 27.8 %all-to-all-start.3 = ((f32[4,1408,88]{1,2,0:T(8,128)}), f32[4,1408,88]{1,2,0:T(8,128)S(1)}, u32[]{:S(2)}, u32[]{:S(2)}) async-start(f32[4,1408,88]{1,2,0:T(8,128)} %broadcast_select_fusion), calls=%async_computation.3 | async-start | bytes 3964928 | tf_op jit(solution)/shard_map/all_to_all | solution.py:96
Sparse Core Ops, SparseCore 0:
  53.1 64.7 all-gather.5
  119.7 26.4 all-gather.7
  700.7 137.5 all-gather.9
  841.7 84.3 all-gather.11
where the time goes:
time: 954 us; the launch traced here: 948 us
  other arithmetic  412 us (43%)
  waiting for transfers between devices  296 us (31%)
  matrix products  92.9 us (10%)
  local copies, waits for them, and re-layouts  76.6 us (8%)
  blocking collectives  26 us (3%)
  between operations  24 us (3%)
  starting transfers between devices  20.6 us (2%)
    another operation x46, other arithmetic, local(): factor_low = jnp.linalg.cholesky(gathered)  264 us
    all_gather x1, waiting for transfers between devices, local(): row_block = lax.all_gather(own_rows, COL, axis=0, tiled=True)  138 us
    another operation x3, other arithmetic, local(): lax.linalg.triangular_solve(factor_low, below_block, left_side=False, low...  131 us
    all_gather x2, waiting for transfers between devices, gather_in_order(): pieces = lax.all_gather(pieces, axes[k], axis=0, tiled=True)  93 us
    another operation x22, matrix products, local(): factor_low = jnp.linalg.cholesky(gathered)  50.1 us
    another operation x36, local copies, waits for them, and re-layouts  34.6 us
    another operation x23, matrix products, local(): lax.linalg.triangular_solve(factor_low, below_block, left_side=False, low...  28.4 us
    all_to_all x1, waiting for transfers between devices, local(): lax.all_to_all(trailing, 'sub', split_axis=2, concat_axis=0, tiled=True)  22.9 us
  transfers between devices with their start and end apart: 8, of which 8 were waited for; matrix products, arithmetic and copies ran while one was open for 1% of the time, Pallas kernels for 0%

commit v1 on v0

--- a/solution.py
+++ b/solution.py
@@ -107,7 +107,9 @@
     own_rows = lax.linalg.triangular_solve(
         factor_low, below_block, left_side=False, lower=True, transpose_a=True
     )
-    row_block = lax.all_gather(own_rows, COL, axis=0, tiled=True)
+    row_block = jnp.concatenate(
+        lax.all_to_all(jnp.stack([own_rows] * lax.axis_size(COL)), COL, 0, 0), axis=0
+    )
     col_block = column_rows(
         row_block,
         rows_count,

time: 954 us -> 1020 us (1.069)
  waiting for transfers between devices: 296 us -> 355 us
  starting transfers between devices: 20.6 us -> 34.1 us
    all_to_all x0 -> x1, waiting for transfers between devices: none -> 198 us  [local(): lax.all_to_all(jnp.stack([own_rows] * lax.axis_size(COL)), COL, 0, 0)]
    all_gather x1 -> x0, waiting for transfers between devices: 138 us -> none  [local(): row_block = lax.all_gather(own_rows, COL, axis=0, tiled=True)]
    another operation x36 -> x37, local copies, waits for them, and re-layouts: 34.6 us -> 39.1 us
where the time goes in v1:
time: 1020 us
  other arithmetic  412 us (40%)
  waiting for transfers between devices  355 us (35%)
  matrix products  84.4 us (8%)
  local copies, waits for them, and re-layouts  80.2 us (8%)
  starting transfers between devices  34.1 us (3%)
  blocking collectives  26 us (3%)
  between operations  24 us (2%)
    another operation x46, other arithmetic, local(): factor_low = jnp.linalg.cholesky(gathered)  264 us
    all_to_all x1, waiting for transfers between devices, local(): lax.all_to_all(jnp.stack([own_rows] * lax.axis_size(COL)), COL, 0, 0)  198 us
    another operation x3, other arithmetic, local(): lax.linalg.triangular_solve(factor_low, below_block, left_side=False, low...  131 us
    all_gather x2, waiting for transfers between devices, gather_in_order(): pieces = lax.all_gather(pieces, axes[k], axis=0, tiled=True)  93.1 us
    another operation x22, matrix products, local(): factor_low = jnp.linalg.cholesky(gathered)  50.1 us
    another operation x36, local copies, waits for them, and re-layouts  34.6 us
    all_to_all x1, waiting for transfers between devices, local(): lax.all_to_all(trailing, 'sub', split_axis=2, concat_axis=0, tiled=True)  22.9 us
    all_to_all x1, waiting for transfers between devices, local(): lax.all_to_all(ordered[2], 'sub', split_axis=0, concat_axis=2, tiled=True)  21.3 us
  transfers between devices with their start and end apart: 8, of which 8 were waited for; matrix products, arithmetic and copies ran while one was open for 1% of the time, Pallas kernels for 0%

profile of v1, /device:TPU:1, one launch (start us, length us, event | category | flops | bytes accessed | tf_op | source)
XLA Modules:
  0.0 1016.3 jit_solution(13058286583577488880)
XLA Ops:
  10.0 4.8 all-to-all-start
  15.7 9.5 all-to-all-done
  26.8 10.4 %all_to_all.80 = f32[4,112,384]{2,1,0:T(8,128)S(1)} all-to-all(f32[4,112,384]{2,1,0:T(8,128)S(1)} %pad_maximum_fusion.1), channel_id=1, replica_groups=mesh['sub'=4,'row_0'=2,'row_1'=2,'col_0'=8,'col_1'=2] {'sub'}, dimensions={0} | all-to-all | bytes 1376256 | tf_op jit(solution)/shard_map/all_to_all | solution.py:31
  37.4 8.7 all_gather.18
  46.1 6.8 all_gather.19
  53.0 64.9 %all-gather.5.cloned.1.call-done = f32[32,24,1536]{2,1,0:T(8,128)} async-done(((f32[4,24,1536]{2,1,0:T(8,128)}), f32[32,24,1536]{2,1,0:T(8,128)}) %all-gather.5.cloned.1.call-update) | async-done | bytes 4718608 | tf_op jit(solution)/shard_map/all_gather | solution.py:47
  117.9 28.2 %all-gather.7.cloned.1.call-done = f32[64,24,1536]{2,1,0:T(8,128)} async-done(((f32[32,24,1536]{2,1,0:T(8,128)}), f32[64,24,1536]{2,1,0:T(8,128)}) %all-gather.7.cloned.1.call-update) | async-done | bytes 9437200 | tf_op jit(solution)/shard_map/all_gather | solution.py:47
  146.2 8.8 copy.42
  155.0 10.1 copy.43
  165.1 12.3 %fusion = f32[1536,1536]{1,0:T(8,128)} fusion(f32[1536,1536]{0,1:T(8,128)} %copy.43, f32[2,2,8,2,24,1536]{5,4,3,2,1,0:T(8,128)} %copy.42), kind=kLoop, calls=%fused_computation.6 | loop fusion | flops 4718592 | bytes 28311552 | tf_op jit(solution)/shard_map/jit(cholesky)/div | solution.py:102
  178.2 11.7 %cholesky.341 = f32[128,128]{1,0:T(8,128)S(1)} custom-call(f32[128,128]{1,0:T(8,128)S(1)} %cholesky.892), custom_call_target="Cholesky" | custom-call | tf_op jit(solution)/shard_map/jit(cholesky)/cholesky | solution.py:102
  190.0 4.9 cholesky.371
  194.9 9.8 custom-call.94
  209.4 11.9 %cholesky.362 = f32[128,128]{1,0:T(8,128)S(1)} custom-call(f32[128,128]{1,0:T(8,128)S(1)} %cholesky.896), custom_call_target="Cholesky" | custom-call | tf_op jit(solution)/shard_map/jit(cholesky)/cholesky | solution.py:102
  221.9 9.8 custom-call.95
  236.1 11.7 %cholesky.385 = f32[128,128]{1,0:T(8,128)S(1)} custom-call(f32[128,128]{1,0:T(8,128)S(1)} %cholesky.901), custom_call_target="Cholesky" | custom-call | tf_op jit(solution)/shard_map/jit(cholesky)/cholesky | solution.py:102
  248.5 10.0 custom-call.96
  263.3 11.7 %cholesky.715 = f32[128,128]{1,0:T(8,128)S(1)} custom-call(f32[128,128]{1,0:T(8,128)S(1)} %cholesky.906), custom_call_target="Cholesky" | custom-call | tf_op jit(solution)/shard_map/jit(cholesky)/cholesky | solution.py:102
  275.7 9.8 custom-call.97
  290.6 12.1 %cholesky.734 = f32[128,128]{1,0:T(8,128)S(1)} custom-call(f32[128,128]{1,0:T(8,128)S(1)} %cholesky.911), custom_call_target="Cholesky" | custom-call | tf_op jit(solution)/shard_map/jit(cholesky)/cholesky | solution.py:102
  303.3 9.8 custom-call.98
  318.4 11.7 %cholesky.754 = f32[128,128]{1,0:T(8,128)S(1)} custom-call(f32[128,128]{1,0:T(8,128)S(1)} %cholesky.916), custom_call_target="Cholesky" | custom-call | tf_op jit(solution)/shard_map/jit(cholesky)/cholesky | solution.py:102
  330.7 10.0 custom-call.99
  345.8 11.7 %cholesky.774 = f32[128,128]{1,0:T(8,128)S(1)} custom-call(f32[128,128]{1,0:T(8,128)S(1)} %cholesky.921), custom_call_target="Cholesky" | custom-call | tf_op jit(solution)/shard_map/jit(cholesky)/cholesky | solution.py:102
  358.1 9.8 custom-call.100
  369.1 4.0 fusion.30
  373.2 11.7 %cholesky.794 = f32[128,128]{1,0:T(8,128)S(1)} custom-call(f32[128,128]{1,0:T(8,128)S(1)} %cholesky.926), custom_call_target="Cholesky" | custom-call | tf_op jit(solution)/shard_map/jit(cholesky)/cholesky | solution.py:102
  385.5 9.8 custom-call.101
  400.1 12.1 %cholesky.814 = f32[128,128]{1,0:T(8,128)S(1)} custom-call(f32[128,128]{1,0:T(8,128)S(1)} %cholesky.931), custom_call_target="Cholesky" | custom-call | tf_op jit(solution)/shard_map/jit(cholesky)/cholesky | solution.py:102
  412.8 9.8 custom-call.102
  426.9 11.7 %cholesky.834 = f32[128,128]{1,0:T(8,128)S(1)} custom-call(f32[128,128]{1,0:T(8,128)S(1)} %cholesky.936), custom_call_target="Cholesky" | custom-call | tf_op jit(solution)/shard_map/jit(cholesky)/cholesky | solution.py:102
  439.3 9.8 custom-call.103
  452.8 11.9 %cholesky.854 = f32[128,128]{1,0:T(8,128)S(1)} custom-call(f32[128,128]{1,0:T(8,128)S(1)} %cholesky.941), custom_call_target="Cholesky" | custom-call | tf_op jit(solution)/shard_map/jit(cholesky)/cholesky | solution.py:102
  465.3 9.8 custom-call.104
  478.2 11.7 %cholesky.872 = f32[128,128]{1,0:T(8,128)S(1)} custom-call(f32[128,128]{1,0:T(8,128)S(1)} %convolution_subtract_fusion.4), custom_call_target="Cholesky" | custom-call | tf_op jit(solution)/shard_map/jit(cholesky)/cholesky | solution.py:102
  505.4 13.0 %fusion.1 = (f32[1536,1536]{1,0:T(8,128)}, f32[1536,1536]{1,0:T(8,128)}) fusion(f32[1536,1536]{1,0:T(8,128)} %get-tuple-element.25, pred[]{:T(512)S(6)} %cholesky.891), kind=kLoop, calls=%fused_computation.9 | loop fusion | flops 9437184 | bytes 28311552 | tf_op jit(solution)/shard_map/triangular_solve | solution.py:107
  518.4 34.8 %while.1 = (s32[]{:T(128)}, f32[1536,1536]{1,0:T(8,128)}, s32[12,2]{0,1:T(2,128)S(1)}, f32[12,128,128]{2,1,0:T(8,128)S(1)}, s32[]{:T(128)}) while((s32[]{:T(128)}, f32[1536,1536]{1,0:T(8,128)}, s32[12,2]{0,1:T(2,128)S(1)}, f32[12,128,128]{2,1,0:T(8,128)S(1)}, s32[]{:T(128)}) %tuple.108), condition=%wide.while_cond, body=%wide.while_body.sunk | while | flops 2 | bytes 131189 | solution.py:107
  553.3 117.9 %custom-call.105 = f32[12,128,128]{1,2,0:T(8,128)S(1)} custom-call(f32[12,128,128]{2,1,0:T(8,128)S(1)} %get-tuple-element.11), custom_call_target="InvertDiagBlocksLowerTriangular" | custom-call | tf_op jit(solution)/shard_map/triangular_solve | solution.py:107
  691.2 4.5 stack.2
  695.7 9.2 all-to-all-start.4
  705.0 197.9 %all-to-all-done.4 = f32[16,88,1536]{2,1,0:T(8,128)} async-done(((f32[16,88,1536]{2,1,0:T(8,128)}), f32[16,88,1536]{2,1,0:T(8,128)}, u32[]{:S(2)}, u32[]{:S(2)}) %all-to-all-start.4) | async-done | bytes 8650784 | tf_op jit(solution)/shard_map/all_to_all | solution.py:111
  909.5 4.0 all-to-all-start.2
  914.1 22.9 %all-to-all-done.2 = f32[1,1408,352]{1,0,2:T(1,128)S(1)} async-done(((f32[1,1408,352]{1,0,2:T(1,128)}), f32[1,1408,352]{1,0,2:T(1,128)S(1)}, u32[]{:S(2)}, u32[]{:S(2)}) %all-to-all-start.2) | async-done | bytes 1982496 | tf_op jit(solution)/shard_map/all_to_all | solution.py:87
  938.3 12.4 %all-to-all-start.5 = ((f32[64,1,1]{2,1,0:T(1,128)}), f32[64,1,1]{2,1,0:T(1,128)S(1)}, u32[]{:S(2)}, u32[]{:S(2)}) async-start(f32[64,1,1]{2,1,0:T(1,128)} %broadcast_in_dim.56), calls=%async_computation.5 | async-start | bytes 65536 | tf_op jit(solution)/shard_map/all_to_all | solution.py:15
  955.8 3.9 all-to-all-done.5
  966.2 21.3 %all-to-all-done.3 = f32[4,1408,88]{1,2,0:T(8,128)S(1)} async-done(((f32[4,1408,88]{1,2,0:T(8,128)}), f32[4,1408,88]{1,2,0:T(8,128)S(1)}, u32[]{:S(2)}, u32[]{:S(2)}) %all-to-all-start.3) | async-done | bytes 1982496 | tf_op jit(solution)/shard_map/all_to_all | solution.py:96
  987.5 6.4 all-gather.9.cloned.1.call-done
  994.0 14.4 %fusion.2 = f32[1,1408,352]{1,2,0:T(8,128)} fusion(f32[1408,352]{0,1:T(8,128)S(1)} %bitcast.194, f32[1408,1536]{1,0:T(8,128)} %bitcast.54, f32[4,352,1536]{2,1,0:T(8,128)} %bitcast.204, s32[]{:T(128)S(6)} %select_n.67), kind=kOutput, calls=%fused_computation.11 | convolution fusion | flops 9135689728 | bytes 14778372 | tf_op jit(solution)/shard_map/dot_general | solution.py:120
  (156 shorter events, 140.9 us)
Async XLA Ops:
  10.0 15.1 %all-to-all-start = ((f32[1,112,1536]{1,0,2:T(1,128)}), f32[1,112,1536]{1,0,2:T(1,128)S(1)}, u32[]{:S(2)}, u32[]{:S(2)}) async-start(f32[1,112,1536]{1,0,2:T(1,128)} %copy.38), calls=%async_computation | async-start | bytes 1572864 | tf_op jit(solution)/shard_map/all_to_all | solution.py:31
  14.8 103.0 %all-gather.5.cloned.1.call-start = ((), (), s32[]{:S(2)}) async-start(), calls=%async_computation.6 | async-start | bytes 5308416 | tf_op jit(solution)/shard_map/all_gather | solution.py:47
  52.9 93.2 %all-gather.7.cloned.1.call-start = ((), (), s32[]{:S(2)}) async-start(), calls=%async_computation.7 | async-start | bytes 14155776 | tf_op jit(solution)/shard_map/all_gather | solution.py:47
  691.1 4.5 copy-start.1
  695.7 210.5 %copy-start = (f32[1,1408,352]{1,2,0:T(8,128)S(1)}, f32[1,1408,352]{1,2,0:T(8,128)}, u32[]{:S(2)}) copy-start(f32[1,1408,352]{1,2,0:T(8,128)} %param.9) | copy-start | bytes 5947396
  695.7 207.2 %all-to-all-start.4 = ((f32[16,88,1536]{2,1,0:T(8,128)}), f32[16,88,1536]{2,1,0:T(8,128)}, u32[]{:S(2)}, u32[]{:S(2)}) async-start(f32[16,88,1536]{2,1,0:T(8,128)} %stack.2), calls=%async_computation.4 | async-start | bytes 17301504 | tf_op jit(solution)/shard_map/all_to_all | solution.py:111
  704.9 208.6 %copy-start.2 = (s32[2]{0:T(128)S(1)}, s32[2]{0:T(128)}, u32[]{:S(2)}) copy-start(s32[2]{0:T(128)} %param.5) | copy-start | bytes 28
  704.9 289.1 %all-gather.9.cloned.1.call-start = ((), (), s32[]{:S(2)}) async-start(), calls=%async_computation.8 | async-start | bytes 10813440 | tf_op jit(solution)/shard_map/all_gather | solution.py:59
  909.5 27.6 %all-to-all-start.2 = ((f32[1,1408,352]{1,0,2:T(1,128)}), f32[1,1408,352]{1,0,2:T(1,128)S(1)}, u32[]{:S(2)}, u32[]{:S(2)}) async-start(f32[1,1408,352]{1,0,2:T(1,128)} %copy.44), calls=%async_computation.2 | async-start | bytes 3964928 | tf_op jit(solution)/shard_map/all_to_all | solution.py:87
  938.3 21.4 %all-to-all-start.5 = ((f32[64,1,1]{2,1,0:T(1,128)}), f32[64,1,1]{2,1,0:T(1,128)S(1)}, u32[]{:S(2)}, u32[]{:S(2)}) async-start(f32[64,1,1]{2,1,0:T(1,128)} %broadcast_in_dim.56), calls=%async_computation.5 | async-start | bytes 65536 | tf_op jit(solution)/shard_map/all_to_all | solution.py:15
  959.7 27.9 %all-to-all-start.3 = ((f32[4,1408,88]{1,2,0:T(8,128)}), f32[4,1408,88]{1,2,0:T(8,128)S(1)}, u32[]{:S(2)}, u32[]{:S(2)}) async-start(f32[4,1408,88]{1,2,0:T(8,128)} %broadcast_select_fusion), calls=%async_computation.3 | async-start | bytes 3964928 | tf_op jit(solution)/shard_map/all_to_all | solution.py:96
Sparse Core Ops, SparseCore 0:
  53.1 64.7 all-gather.4
  119.7 26.4 all-gather.6
  906.3 87.6 all-gather.8
